TPU v7x, 16 devices: a 4x2x1 block of a 4x4x8 slice. The times are simulated.
16 devices in a mesh: rep: 2 (over y, z), dp: 8 (over x, core).
Axes of the slice: x: 4, y: 2, z: 1, core: 2. Of those that a mesh axis runs over, the one named last changes fastest.
The devices are a block of a 4x4x8 slice.
Arguments:
- a: bfloat16 [16, 4, 4096, 640], P(('rep', 'dp')), parts along dimension 0
- g: bfloat16 [16, 4, 4096, 1536], P(('rep', 'dp')), parts along dimension 0
Outputs:
- output: bfloat16 [8, 640, 1536], P('rep'), parts along dimension 0
There are 2 independent parts. A program takes and returns all parts, laid end to end along the dimension named above; each array names one.
All inputs are finite; a program needn't handle non-finite values.
Results may differ from a plain program's by a relative error of at most 0.012.
Values are sent between devices in bfloat16 or wider.
A program may use at most 768 MiB of HBM per device.

v0:
```python
import jax
import jax.numpy as jnp


def solution(mesh):
    groups = mesh.shape["rep"]

    def step(a, g):
        a, g = (t.reshape(groups, -1, *t.shape[1:]) for t in (a, g))
        sums = jnp.einsum("rsntd,rsntf->rndf", a, g, preferred_element_type=jnp.float32)
        return sums.astype(jnp.bfloat16).reshape(-1, *sums.shape[2:])

    return step
```

profile of v0, /device:TPU:113, one launch (start us, length us, event | category | flops | bytes accessed | tf_op | source)
XLA Modules:
  0.0 205.4 jit_solution(15365151294358377734)
XLA Ops:
  0.0 41.6 %fusion.3 = f32[1,4,640,1536]{3,2,1,0:T(8,128)} fusion(bf16[1,4,4096,1536]{3,2,1,0:T(8,128)(2,1)} %param.1, bf16[1,4,4096,640]{3,2,1,0:T(8,128)(2,1)} %param), kind=kOutput, calls=%fused_computation.4 | convolution fusion | flops 32212254720 | bytes 87031808 | tf_op jit(solution)/rsntd,rsntf->rndf/dot_general | solution.py:10
  41.6 163.8 %all-reduce.2 = bf16[1,4,640,1536]{3,2,1,0:T(8,128)(2,1)} all-reduce(f32[1,4,640,1536]{3,2,1,0:T(8,128)} %fusion.3), channel_id=1, replica_groups=[2,8]<=[16], use_global_device_ids=true, to_apply=%add.clone | all-reduce | flops 3932160 | bytes 23592960 | tf_op jit(solution)/rsntd,rsntf->rndf/dot_general | solution.py:10
where the time goes:
time: 207 us; the launch traced here: 205 us
  blocking collectives  164 us (79%)
  matrix products  41.6 us (20%)
    dot_general x1, blocking collectives, step(): jnp.einsum('rsntd,rsntf->rndf', a, g, preferred_element_type=jnp.float32)  164 us
    dot_general x1, matrix products, step(): jnp.einsum('rsntd,rsntf->rndf', a, g, preferred_element_type=jnp.float32)  41.6 us

commit v1 on v0

v1 whole, which is shorter than its diff:
```python
import functools

import jax
import jax.numpy as jnp
from jax import lax
from jax.experimental import pallas as pl
from jax.experimental.pallas import tpu as pltpu
from jax.sharding import PartitionSpec as P

MESH = pl.DeviceIdType.MESH
CORES = 2
NB = 256
KC = 1024
AS = 4
RW = 3
DS = 4


def kernel(
    chips, a_hbm, g_hbm, out, at, a_stage, g_buf, own, d_send, d_recv, r_send, r_recv,
    a_sem, g_sem, ds_sem, dr_sem, rs_sem, rr_sem, fs_sem, fr_sem,
):
    matrices, tokens, d = a_hbm.shape
    ff = g_hbm.shape[2]
    half = d // CORES
    per_matrix = ff // NB
    rounds = matrices * per_matrix // chips
    steps = rounds * chips
    per_wave = RW * chips
    mats_per_wave = per_wave // per_matrix
    blocks = tokens // KC

    me = lax.axis_index("dp")
    chip, core = me // CORES, lax.rem(me, CORES)
    way = 1 - 2 * core
    peer = chip * CORES + 1 - core
    right = lax.rem(chip + way + chips, chips) * CORES + core
    left = lax.rem(chip - way + chips, chips) * CORES + core
    my_rows = pl.ds(pl.multiple_of(core * half, half), half)

    def mine(j):
        return lax.rem(chip - 1 - way * j + chips * chips, chips)

    def peers(j):
        return lax.rem(chip - 1 + way * j + chips * chips, chips)

    def place(r, ch):
        c = r * chips + ch
        return c // per_matrix, pl.ds(pl.multiple_of(lax.rem(c, per_matrix) * NB, NB), NB)

    def load_a(m, b):
        slot = b % AS
        return pltpu.make_async_copy(a_hbm.at[m, pl.ds(b * KC, KC), :], a_stage.at[slot], a_sem.at[slot])

    def load_g(r, ch):
        n, cols = place(r, ch)
        slot = lax.rem(r, RW) * chips + ch
        return pltpu.make_async_copy(g_hbm.at[n, :, cols], g_buf.at[slot], g_sem.at[slot])

    def swap(i):
        return pltpu.make_async_remote_copy(
            src_ref=d_send.at[lax.rem(i, DS)], dst_ref=d_recv.at[i],
            send_sem=ds_sem.at[lax.rem(i, DS)], recv_sem=dr_sem.at[i],
            device_id={"dp": peer}, device_id_type=MESH)

    def reduce_hop(r, j):
        k = r * (chips - 1) + j
        return pltpu.make_async_remote_copy(
            src_ref=r_send.at[k], dst_ref=r_recv.at[k], send_sem=rs_sem.at[r * chips * 2 + j],
            recv_sem=rr_sem.at[r * chips * 2 + j], device_id={"dp": right}, device_id_type=MESH)

    def gather_hop(r, t, ch):
        n, cols = place(r, ch)
        k = r * chips * 2 + chips + t
        return pltpu.make_async_remote_copy(
            src_ref=out.at[n, my_rows, cols], dst_ref=out.at[n, my_rows, cols], send_sem=rs_sem.at[k],
            recv_sem=rr_sem.at[k], device_id={"dp": right}, device_id_type=MESH)

    def hand_over(r, t, ch):
        n, cols = place(r, ch)
        k = r * chips + t
        return pltpu.make_async_remote_copy(
            src_ref=out.at[n, my_rows, cols], dst_ref=out.at[n, my_rows, cols], send_sem=fs_sem.at[k],
            recv_sem=fr_sem.at[k], device_id={"dp": peer}, device_id_type=MESH)

    load_g(0, mine(0)).start()
    for b in range(AS):
        load_a(0, b).start()

    barrier = pltpu.get_barrier_semaphore()
    for other in (left, right, peer):
        pl.semaphore_signal(barrier, inc=1, device_id={"dp": other}, device_id_type=MESH)
    pl.semaphore_wait(barrier, 3)

    def first_loads():
        for j in range(chips):
            for r in range(RW):
                if r or j:
                    load_g(r, lax.rem(chip - 1 + j + chips, chips)).start()

    def transpose(m):
        for b in range(blocks):
            load_a(m, b).wait()
            at[lax.rem(m, mats_per_wave), :, b * KC:(b + 1) * KC] = a_stage[b % AS].T

            @pl.when(m + 1 < matrices)
            def _():
                load_a(m + 1, b).start()

    def combine(i):
        w, ii = i // per_wave, lax.rem(i, per_wave)
        j, r = ii // RW, w * RW + lax.rem(ii, RW)
        swap(i).wait_recv()
        both = own.at[lax.rem(i, 2)]

        @pl.when(j == 0)
        def _():
            r_send[r * (chips - 1)] = (both[...] + d_recv[i].astype(jnp.float32)).astype(jnp.bfloat16)
            reduce_hop(r, 0).start()

        @pl.when(j > 0)
        def _():
            reduce_hop(r, j - 1).wait_recv()
            total = both[...] + d_recv[i].astype(jnp.float32)
            total += r_recv[r * (chips - 1) + j - 1].astype(jnp.float32)
            both[...] = total

        @pl.when((j > 0) & (j < chips - 1))
        def _():
            r_send[r * (chips - 1) + j] = both[...].astype(jnp.bfloat16)
            reduce_hop(r, j).start()

        @pl.when(j == chips - 1)
        def _():
            n, cols = place(r, mine(chips - 1))
            out[n, my_rows, cols] = both[...].astype(jnp.bfloat16)
            gather_hop(r, 0, mine(chips - 1)).start()
            hand_over(r, chips - 1, mine(chips - 1)).start()

    def forward(w, x):
        t, r = x // RW, w * RW + lax.rem(x, RW)
        ch = mine(t)
        gather_hop(r, t, ch).wait_recv()

        @pl.when(t < chips - 2)
        def _():
            gather_hop(r, t + 1, ch).start()

        hand_over(r, t, ch).start()

    def step(i, carry):
        w, ii = i // per_wave, lax.rem(i, per_wave)
        j, r = ii // RW, w * RW + lax.rem(ii, RW)

        @pl.when(ii < mats_per_wave)
        def _():
            transpose(w * mats_per_wave + ii)

        @pl.when(i == 0)
        def _():
            first_loads()

        seen = set()
        for jj in range(chips):
            new = [s for s in {(jj % chips), (-jj) % chips} if s not in seen]
            seen.update(new)
            if new:
                @pl.when(j == jj)
                def _():
                    for s in new:
                        load_g(r, lax.rem(chip - 1 + s + chips, chips)).wait()

        def unit(u, carry):
            ch = jnp.where(u == 0, peers(j), mine(j))
            rows = jnp.where(u == 0, 1 - core, core) * half
            m = (r * chips + ch) // per_matrix
            lhs = at[lax.rem(m, mats_per_wave), pl.ds(pl.multiple_of(rows, half), half), :]
            rhs = g_buf[lax.rem(r, RW) * chips + ch]
            own[jnp.where(u == 0, 2, lax.rem(i, 2))] = jnp.dot(lhs, rhs, preferred_element_type=jnp.float32)

            @pl.when(u == 0)
            def _():
                @pl.when(i >= DS)
                def _():
                    swap(i - DS).wait_send()

                d_send[lax.rem(i, DS)] = own[2].astype(jnp.bfloat16)
                swap(i).start()

                @pl.when(i > 0)
                def _():
                    combine(i - 1)

                @pl.when((w > 0) & (ii < per_wave - RW))
                def _():
                    forward(w - 1, ii)

            return carry

        lax.fori_loop(0, CORES, unit, 0)

        last = {}
        for jj in range(chips):
            for s in {(jj % chips), (-jj) % chips}:
                last[s] = jj
        for jj in range(chips):
            done = [s for s in last if last[s] == jj]
            if done:
                @pl.when((j == jj) & (r + RW < rounds))
                def _():
                    for s in done:
                        load_g(r + RW, lax.rem(chip - 1 + s + chips, chips)).start()

        return carry

    lax.fori_loop(0, steps, step, 0)
    combine(steps - 1)

    waves = steps // per_wave

    def rest(x, carry):
        forward(waves - 1, x)
        return carry

    lax.fori_loop(0, per_wave - RW, rest, 0)

    for i in range(steps - DS, steps):
        swap(i).wait_send()

    def settle(r, carry):
        for j in range(chips - 1):
            reduce_hop(r, j).wait_send()
        for t in range(chips - 1):
            gather_hop(r, t, 0).wait_send()
        for t in range(chips):
            hand_over(r, t, 0).wait()
        return carry

    lax.fori_loop(0, rounds, settle, 0)


def solution(mesh):
    chips = mesh.shape["dp"] // CORES

    def one(a, g):
        a, g = a[0], g[0]
        matrices, tokens, d = a.shape
        ff = g.shape[2]
        half = d // CORES
        steps = matrices * ff // NB
        rounds = steps // chips
        dma = pltpu.SemaphoreType.DMA
        bf16, f32 = jnp.bfloat16, jnp.float32
        return pl.pallas_call(
            functools.partial(kernel, chips),
            out_shape=OUT((matrices, d, ff), bf16) if OUT else jax.ShapeDtypeStruct((matrices, d, ff), bf16),
            in_specs=[pl.BlockSpec(memory_space=pltpu.MemorySpace.HBM)] * 2,
            out_specs=pl.BlockSpec(memory_space=pltpu.MemorySpace.VMEM),
            scratch_shapes=[
                pltpu.VMEM((RW * chips * NB // ff, d, tokens), bf16),
                pltpu.VMEM((AS, KC, d), bf16),
                pltpu.VMEM((RW * chips, tokens, NB), bf16),
                pltpu.VMEM((3, half, NB), f32),
                pltpu.VMEM((DS, half, NB), bf16),
                pltpu.VMEM((steps, half, NB), bf16),
                pltpu.VMEM((rounds * (chips - 1), half, NB), bf16),
                pltpu.VMEM((rounds * (chips - 1), half, NB), bf16),
                dma((AS,)), dma((RW * chips,)), dma((DS,)), dma((steps,)),
                dma((rounds * chips * 2,)), dma((rounds * chips * 2,)), dma((steps,)), dma((steps,)),
            ],
            compiler_params=pltpu.CompilerParams(
                collective_id=0, has_side_effects=True, vmem_limit_bytes=VMEM_LIMIT),
        )(a, g)

    return jax.shard_map(
        one, mesh=mesh, in_specs=(P(("rep", "dp")),) * 2, out_specs=P("rep"), check_vma=False)


OUT = pltpu.MemorySpace.VMEM
VMEM_LIMIT = 53 * 2**20
```

time: 207 us -> 87.5 us (0.42)
  blocking collectives: 164 us -> 0 us
  Pallas kernels: 0 us -> 84.2 us
  matrix products: 41.6 us -> 0 us
  local copies, waits for them, and re-layouts: 0 us -> 3.22 us
    dot_general x1 -> x0, blocking collectives: 164 us -> none  [step(): jnp.einsum('rsntd,rsntf->rndf', a, g, preferred_element_type=jnp.float32)]
    pallas_call x0 -> x1, Pallas kernels: none -> 84.2 us  [one(): pl.pallas_call(functools.partial(kernel, chips), out_shape=OUT((matrices,...]
    dot_general x1 -> x0, matrix products: 41.6 us -> none  [step(): jnp.einsum('rsntd,rsntf->rndf', a, g, preferred_element_type=jnp.float32)]
    unnamed x0 -> x1, local copies, waits for them, and re-layouts: none -> 3.22 us
where the time goes in v1:
time: 87.5 us; the launch traced here: 87.4 us
  Pallas kernels  84.2 us (96%)
  local copies, waits for them, and re-layouts  3.22 us (4%)
    pallas_call x1, Pallas kernels, one(): pl.pallas_call(functools.partial(kernel, chips), out_shape=OUT((matrices,...  84.2 us
    unnamed x1, local copies, waits for them, and re-layouts  3.22 us

profile of v1, /device:TPU:113, one launch (start us, length us, event | category | flops | bytes accessed | tf_op | source)
XLA Modules:
  0.0 87.4 jit_solution(12819444886212521383)
XLA Ops:
  0.0 84.2 %shard_map.28 = bf16[4,640,1536]{2,1,0:T(8,128)(2,1)S(1)} custom-call(bf16[4,4096,640]{2,1,0:T(8,128)(2,1)} %bitcast.3, bf16[4,4096,1536]{2,1,0:T(8,128)(2,1)} %bitcast.2), custom_call_target="tpu_custom_call" | custom-call | tf_op jit(solution)/shard_map/pallas_call | solution.py:254
  84.2 3.2 %copy.4 = bf16[4,640,1536]{2,1,0:T(8,128)(2,1)} copy(bf16[4,640,1536]{2,1,0:T(8,128)(2,1)S(1)} %shard_map.28) | data formatting | bytes 15728640

commit v2 on v0

v2 whole, which is shorter than its diff:
```python
import functools

import jax
import jax.numpy as jnp
from jax import lax
from jax.experimental import pallas as pl
from jax.experimental.pallas import tpu as pltpu
from jax.sharding import PartitionSpec as P

MESH = pl.DeviceIdType.MESH
CORES = 2
NB = 256
AS = 4
AM = 2
RW = 3
DS = 4


def kernel(
    chips, a_hbm, g_hbm, out, at, a_stage, g_buf, whole, own, d_send, d_recv, r_send, r_recv,
    a_sem, h_sem, g_sem, ds_sem, dr_sem, rs_sem, gs_sem, rr_sem, fs_sem, fr_sem,
):
    matrices, tokens, d = a_hbm.shape
    ff = g_hbm.shape[2]
    half = d // CORES
    per_matrix = ff // NB
    rounds = matrices * per_matrix // chips
    steps = rounds * chips
    per_wave = RW * chips
    waves = steps // per_wave
    forwards = per_wave - RW
    block = tokens // AS
    f32, bf16 = jnp.float32, jnp.bfloat16

    me = lax.axis_index("dp")
    chip, core = me // CORES, lax.rem(me, CORES)
    way = 1 - 2 * core
    peer = chip * CORES + 1 - core
    right = lax.rem(chip + way + chips, chips) * CORES + core
    left = lax.rem(chip - way + chips, chips) * CORES + core

    def rows(c):
        return pl.ds(pl.multiple_of(c * half, half), half)

    my_rows, peer_rows = rows(core), rows(1 - core)

    def nth(s):
        return lax.rem(chip - 1 + s + chips * chips, chips)

    def mine(j):
        return nth(-way * j)

    def peers(j):
        return nth(way * j)

    def split(i):
        w, ii = i // per_wave, lax.rem(i, per_wave)
        return ii // RW, w * RW + lax.rem(ii, RW)

    def place(r, ch):
        c = r * chips + ch
        return c // per_matrix, pl.ds(pl.multiple_of(lax.rem(c, per_matrix) * NB, NB), NB)

    def g_slot(r, ch):
        return lax.rem(r, RW) * chips + ch

    def tokens_of(b):
        return pl.ds(pl.multiple_of(b * block, block), block)

    def load_a(m, b):
        return pltpu.make_async_copy(a_hbm.at[m, tokens_of(b), :], a_stage.at[b], a_sem.at[b])

    def load_g(r, ch):
        n, cols = place(r, ch)
        slot = g_slot(r, ch)
        return pltpu.make_async_copy(g_hbm.at[n, :, cols], g_buf.at[slot], g_sem.at[slot])

    def load_first(b):
        n, cols = place(0, nth(0))
        return pltpu.make_async_copy(
            g_hbm.at[n, tokens_of(b), cols], g_buf.at[g_slot(0, nth(0)), tokens_of(b)], h_sem.at[b])

    def to(device, src, dst, send_sem, recv_sem):
        return pltpu.make_async_remote_copy(
            src_ref=src, dst_ref=dst, send_sem=send_sem, recv_sem=recv_sem,
            device_id={"dp": device}, device_id_type=MESH)

    def swap(i):
        s = lax.rem(i, DS)
        return to(peer, d_send.at[s], d_recv.at[s], ds_sem.at[s], dr_sem.at[s])

    def reduce_hop(r, j):
        k = r * (chips - 1) + j
        return to(right, r_send.at[k], r_recv.at[k], rs_sem.at[0], rr_sem.at[r * chips + j])

    def gather_hop(r, t, ch):
        n, cols = place(r, ch)
        at_ = out.at[n, my_rows, cols]
        return to(right, at_, at_, gs_sem.at[0], rr_sem.at[r * chips + lax.rem(t + chips - 1, chips)])

    def hand_over(r, ch):
        n, cols = place(r, ch)
        at_ = out.at[n, my_rows, cols]
        return to(peer, at_, at_, fs_sem.at[0], fr_sem.at[0])

    def transpose(m, b):
        load_a(m, b).wait()
        at[lax.rem(m, AM), :, tokens_of(b)] = a_stage[b].T

        @pl.when(m + 1 < matrices)
        def _():
            load_a(m + 1, b).start()

    def dot(i, ch, which):
        j, r = split(i)
        m = (r * chips + ch) // per_matrix
        return jnp.dot(at[lax.rem(m, AM), which, :], g_buf[g_slot(r, ch)], preferred_element_type=f32)

    def combine(i):
        j, r = split(i)
        s = lax.rem(i, DS)
        swap(i).wait_recv()

        @pl.when(j == 0)
        def _():
            r_send[r * (chips - 1)] = (own[...] + d_recv[s].astype(f32)).astype(bf16)
            reduce_hop(r, 0).start()

        @pl.when(j > 0)
        def _():
            reduce_hop(r, j - 1).wait_recv()
            own[...] = own[...] + d_recv[s].astype(f32) + r_recv[r * (chips - 1) + j - 1].astype(f32)

        @pl.when((j > 0) & (j < chips - 1))
        def _():
            r_send[r * (chips - 1) + j] = own[...].astype(bf16)
            reduce_hop(r, j).start()

        @pl.when(j == chips - 1)
        def _():
            ch = mine(chips - 1)
            n, cols = place(r, ch)
            out[n, my_rows, cols] = own[...].astype(bf16)
            gather_hop(r, 0, ch).start()
            hand_over(r, ch).start()

    def forward(w, x):
        t, r = x // RW, w * RW + lax.rem(x, RW)
        ch = mine(t)
        gather_hop(r, t, ch).wait_recv()

        @pl.when(t < chips - 2)
        def _():
            gather_hop(r, t + 1, ch).start()

        hand_over(r, ch).start()

    def send_peers(i, value):
        d_send[lax.rem(i, DS)] = value.astype(bf16)

    first, last = {}, {}
    for j in range(chips):
        for s in sorted({j, -j % chips}):
            first.setdefault(s, j)
            last[s] = j

    for b in range(AS):
        load_a(0, b).start()
        load_first(b).start()

    barrier = pltpu.get_barrier_semaphore()
    for other in (left, right, peer):
        pl.semaphore_signal(barrier, inc=1, device_id={"dp": other}, device_id_type=MESH)

    always = chip >= 0

    def products(b):
        cols = slice(b * block, (b + 1) * block)
        term = jnp.dot(at[0, :, cols], g_buf[g_slot(0, nth(0)), cols, :], preferred_element_type=f32)
        whole[...] = whole[...] + term if b else term

    for b in range(AS + 1):
        m, k = b // AS, b % AS
        if m == 0:
            load_first(k).wait()
        load_a(m, k).wait()

        @pl.when(always)
        def _():
            at[m, :, k * block:(k + 1) * block] = a_stage[k].T
            if b:
                products(b - 1)

        load_a(m + 1, k).start()
        if 0 < b < RW:
            load_g(b, nth(0)).start()

    send_peers(0, whole[peer_rows, :])
    own[...] = whole[my_rows, :]
    pl.semaphore_wait(barrier, 3)
    swap(0).start()

    for s in sorted(first, key=lambda s: first[s]):
        if s:
            for r in range(RW):
                load_g(r, nth(s)).start()

    for b in range(1, AS):
        transpose(1, b)
        if b == AS - 2:
            combine(0)

    def lone_peers(i, r):
        load_g(r, nth(0)).wait()

        @pl.when(always)
        def _():
            send_peers(i, dot(i, peers(0), peer_rows))

        swap(i).start()

    def lone_mine(i):
        @pl.when(always)
        def _():
            own[...] = dot(i, mine(chips - 1), my_rows)

    def transpose_some(m, begin, end):
        def one(b, carry):
            transpose(m, b)
            return carry

        lax.fori_loop(begin, end, one, 0)

    load_g(RW, nth(0)).start()
    lone_peers(1, 1)

    def step(i, carry):
        w, ii = i // per_wave, lax.rem(i, per_wave)
        j, r = split(i)
        nj, nr = split(i + 1)

        for jj in range(chips):
            new = [s for s in first if first[s] == jj]
            if new:
                @pl.when(nj == jj)
                def _():
                    for s in new:
                        load_g(nr, nth(s)).wait()

        @pl.when(i + 1 >= DS)
        def _():
            swap(i + 1 - DS).wait_send()

        own[...] = dot(i, mine(j), my_rows)
        send_peers(i + 1, dot(i + 1, peers(nj), peer_rows))
        swap(i + 1).start()
        combine(i)

        @pl.when((w > 0) & (ii < forwards - 2))
        def _():
            forward(w - 1, ii + 2)

        for jj in range(chips):
            free = [s for s in last if last[s] == jj]
            if free:
                @pl.when((j == jj) & (r + RW < rounds))
                def _():
                    for s in free:
                        load_g(r + RW, nth(s)).start()

        return carry

    for w in range(waves):
        begin, end = w * per_wave, (w + 1) * per_wave

        if w:
            transpose_some(2 * w, 0, AS)
            forward(w - 1, 0)
            swap(begin - DS).wait_send()
            lone_peers(begin, w * RW)
            transpose_some(2 * w + 1, 0, AS // 2)
            forward(w - 1, 1)
            transpose_some(2 * w + 1, AS // 2, AS)

        lax.fori_loop(begin + (w == 0), end - 1, step, 0)
        lone_mine(end - 1)
        combine(end - 1)
        if w + 1 < waves:
            for q in last:
                if last[q] == chips - 1:
                    load_g((w + 2) * RW - 1, nth(q)).start()

    def rest(x, carry):
        forward(waves - 1, x)
        return carry

    lax.fori_loop(0, forwards, rest, 0)

    for i in range(steps - DS, steps):
        swap(i).wait_send()
    to(right, r_send, r_recv, rs_sem.at[0], rr_sem.at[0]).wait_send()
    to(right, r_send, r_recv, gs_sem.at[0], rr_sem.at[0]).wait_send()
    all_mine = out.at[:, my_rows, :]
    to(peer, all_mine, all_mine, fs_sem.at[0], fr_sem.at[0]).wait()


def solution(mesh):
    chips = mesh.shape["dp"] // CORES

    def one(a, g):
        a, g = a[0], g[0]
        matrices, tokens, d = a.shape
        ff = g.shape[2]
        half = d // CORES
        rounds = matrices * ff // NB // chips
        hops = rounds * (chips - 1)
        bf16, f32 = jnp.bfloat16, jnp.float32
        sems = [AS, AS, RW * chips, DS, DS, 1, 1, rounds * chips, 1, 1]
        return pl.pallas_call(
            functools.partial(kernel, chips),
            out_shape=pltpu.MemorySpace.VMEM((matrices, d, ff), bf16),
            in_specs=[pl.BlockSpec(memory_space=pltpu.MemorySpace.HBM)] * 2,
            out_specs=pl.BlockSpec(memory_space=pltpu.MemorySpace.VMEM),
            scratch_shapes=[
                pltpu.VMEM((AM, d, tokens), bf16),
                pltpu.VMEM((AS, tokens // AS, d), bf16),
                pltpu.VMEM((RW * chips, tokens, NB), bf16),
                pltpu.VMEM((d, NB), f32),
                pltpu.VMEM((half, NB), f32),
                pltpu.VMEM((DS, half, NB), bf16),
                pltpu.VMEM((DS, half, NB), bf16),
                pltpu.VMEM((hops, half, NB), bf16),
                pltpu.VMEM((hops, half, NB), bf16),
                *(pltpu.SemaphoreType.DMA((n,)) for n in sems),
            ],
            compiler_params=pltpu.CompilerParams(
                collective_id=0, has_side_effects=True, vmem_limit_bytes=54 * 2**20),
        )(a, g)

    return jax.shard_map(
        one, mesh=mesh, in_specs=(P(("rep", "dp")),) * 2, out_specs=P("rep"), check_vma=False)
```

time: 207 us -> 81.6 us (0.39)
  blocking collectives: 164 us -> 0 us
  Pallas kernels: 0 us -> 78.3 us
  matrix products: 41.6 us -> 0 us
  local copies, waits for them, and re-layouts: 0 us -> 3.22 us
    dot_general x1 -> x0, blocking collectives: 164 us -> none  [step(): jnp.einsum('rsntd,rsntf->rndf', a, g, preferred_element_type=jnp.float32)]
    pallas_call x0 -> x1, Pallas kernels: none -> 78.3 us  [one(): pl.pallas_call(functools.partial(kernel, chips), out_shape=pltpu.MemorySp...]
    dot_general x1 -> x0, matrix products: 41.6 us -> none  [step(): jnp.einsum('rsntd,rsntf->rndf', a, g, preferred_element_type=jnp.float32)]
    unnamed x0 -> x1, local copies, waits for them, and re-layouts: none -> 3.22 us
where the time goes in v2:
time: 81.6 us
  Pallas kernels  78.3 us (96%)
  local copies, waits for them, and re-layouts  3.22 us (4%)
    pallas_call x1, Pallas kernels, one(): pl.pallas_call(functools.partial(kernel, chips), out_shape=pltpu.MemorySp...  78.3 us
    unnamed x1, local copies, waits for them, and re-layouts  3.22 us

profile of v2, /device:TPU:113, one launch (start us, length us, event | category | flops | bytes accessed | tf_op | source)
XLA Modules:
  0.0 81.6 jit_solution(14683434727792628827)
XLA Ops:
  0.0 78.3 %shard_map.28 = bf16[4,640,1536]{2,1,0:T(8,128)(2,1)S(1)} custom-call(bf16[4,4096,640]{2,1,0:T(8,128)(2,1)} %bitcast.3, bf16[4,4096,1536]{2,1,0:T(8,128)(2,1)} %bitcast.2), custom_call_target="tpu_custom_call" | custom-call | tf_op jit(solution)/shard_map/pallas_call | solution.py:319
  78.3 3.2 %copy.4 = bf16[4,640,1536]{2,1,0:T(8,128)(2,1)} copy(bf16[4,640,1536]{2,1,0:T(8,128)(2,1)S(1)} %shard_map.28) | data formatting | bytes 15728640

commit v3 on v2

--- a/solution.py
+++ b/solution.py
@@ -107,8 +107,7 @@
         load_a(m, b).wait()
         at[lax.rem(m, AM), :, tokens_of(b)] = a_stage[b].T
 
-        @pl.when(m + 1 < matrices)
-        def _():
+        if m % 2 == 0:
             load_a(m + 1, b).start()
 
     def dot(i, ch, which):
@@ -181,9 +180,9 @@
 
     for b in range(AS + 1):
         m, k = b // AS, b % AS
-        if m == 0:
-            load_first(k).wait()
         load_a(m, k).wait()
+        if b < AS:
+            load_first(b).wait()
 
         @pl.when(always)
         def _():
@@ -191,24 +190,28 @@
             if b:
                 products(b - 1)
 
-        load_a(m + 1, k).start()
-        if 0 < b < RW:
-            load_g(b, nth(0)).start()
+        if b < AS:
+            load_a(1, b).start()
+        if b == AS - 1:
+            load_g(1, nth(0)).start()
 
     send_peers(0, whole[peer_rows, :])
     own[...] = whole[my_rows, :]
     pl.semaphore_wait(barrier, 3)
     swap(0).start()
 
-    for s in sorted(first, key=lambda s: first[s]):
-        if s:
-            for r in range(RW):
-                load_g(r, nth(s)).start()
-
     for b in range(1, AS):
-        transpose(1, b)
+        load_a(1, b).wait()
+        at[1, :, b * block:(b + 1) * block] = a_stage[b].T
         if b == AS - 2:
-            combine(0)
+            load_g(2, nth(0)).start()
+
+    combine(0)
+    for j in range(1, chips):
+        for r in range(RW):
+            for s in first:
+                if first[s] == j:
+                    load_g(r, nth(s)).start()
 
     def lone_peers(i, r):
         load_g(r, nth(0)).wait()
@@ -231,7 +234,6 @@
 
         lax.fori_loop(begin, end, one, 0)
 
-    load_g(RW, nth(0)).start()
     lone_peers(1, 1)
 
     def step(i, carry):
@@ -256,12 +258,12 @@
         swap(i + 1).start()
         combine(i)
 
-        @pl.when((w > 0) & (ii < forwards - 2))
-        def _():
-            forward(w - 1, ii + 2)
+        @pl.when((w > 0) & (ii < forwards - 3))
+        def _():
+            forward(w - 1, ii + 3)
 
         for jj in range(chips):
-            free = [s for s in last if last[s] == jj]
+            free = [s for s in last if last[s] == jj > 0]
             if free:
                 @pl.when((j == jj) & (r + RW < rounds))
                 def _():
@@ -281,8 +283,18 @@
             transpose_some(2 * w + 1, 0, AS // 2)
             forward(w - 1, 1)
             transpose_some(2 * w + 1, AS // 2, AS)
-
-        lax.fori_loop(begin + (w == 0), end - 1, step, 0)
+            forward(w - 1, 2)
+
+        begin += w == 0
+        if w + 1 < waves:
+            middle = (begin + end) // 2
+            lax.fori_loop(begin, middle, step, 0)
+            for b in range(AS):
+                load_a(2 * w + 2, b).start()
+            for r in range(RW):
+                load_g((w + 1) * RW + r, nth(0)).start()
+            begin = middle
+        lax.fori_loop(begin, end - 1, step, 0)
         lone_mine(end - 1)
         combine(end - 1)
         if w + 1 < waves:

time: 81.6 us -> 80.6 us (0.988)
  Pallas kernels: 78.3 us -> 77.3 us
    pallas_call x1, Pallas kernels: 78.3 us -> 77.3 us  [one(): pl.pallas_call(functools.partial(kernel, chips), out_shape=pltpu.MemorySp...]
where the time goes in v3:
time: 80.6 us; the launch traced here: 80.5 us
  Pallas kernels  77.3 us (96%)
  local copies, waits for them, and re-layouts  3.22 us (4%)
    pallas_call x1, Pallas kernels, one(): pl.pallas_call(functools.partial(kernel, chips), out_shape=pltpu.MemorySp...  77.3 us
    unnamed x1, local copies, waits for them, and re-layouts  3.22 us

profile of v3, /device:TPU:113, one launch (start us, length us, event | category | flops | bytes accessed | tf_op | source)
XLA Modules:
  0.0 80.5 jit_solution(12951615097150558157)
XLA Ops:
  0.0 77.3 %shard_map.28 = bf16[4,640,1536]{2,1,0:T(8,128)(2,1)S(1)} custom-call(bf16[4,4096,640]{2,1,0:T(8,128)(2,1)} %bitcast.3, bf16[4,4096,1536]{2,1,0:T(8,128)(2,1)} %bitcast.2), custom_call_target="tpu_custom_call" | custom-call | tf_op jit(solution)/shard_map/pallas_call | solution.py:331
  77.3 3.2 %copy.4 = bf16[4,640,1536]{2,1,0:T(8,128)(2,1)} copy(bf16[4,640,1536]{2,1,0:T(8,128)(2,1)S(1)} %shard_map.28) | data formatting | bytes 15728640

commit v4 on v3

--- a/solution.py
+++ b/solution.py
@@ -14,11 +14,12 @@
 AM = 2
 RW = 3
 DS = 4
+NEAR = 240
 
 
 def kernel(
     chips, a_hbm, g_hbm, out, at, a_stage, g_buf, whole, own, d_send, d_recv, r_send, r_recv,
-    a_sem, h_sem, g_sem, ds_sem, dr_sem, rs_sem, gs_sem, rr_sem, fs_sem, fr_sem,
+    a_sem, h_sem, g_sem, ds_sem, dr_sem, rs_sem, gs_sem, rr_sem, xr_sem, fs_sem, fr_sem,
 ):
     matrices, tokens, d = a_hbm.shape
     ff = g_hbm.shape[2]
@@ -98,6 +99,18 @@
         at_ = out.at[n, my_rows, cols]
         return to(right, at_, at_, gs_sem.at[0], rr_sem.at[r * chips + lax.rem(t + chips - 1, chips)])
 
+    final, longer = rounds - 1, core == 0
+
+    def near(ch):
+        n, cols = place(final, ch)
+        at_ = out.at[n, pl.ds(pl.multiple_of(core * half, half), NEAR), cols]
+        return to(left, at_, at_, gs_sem.at[0], xr_sem.at[0])
+
+    def final_hop(ch):
+        n, cols = place(final, ch)
+        at_ = out.at[n, pl.ds(pl.multiple_of(core * half + NEAR, 16), half - NEAR), cols]
+        return to(right, at_, at_, gs_sem.at[0], rr_sem.at[final * chips + chips - 3])
+
     def hand_over(r, ch):
         n, cols = place(r, ch)
         at_ = out.at[n, my_rows, cols]
@@ -143,14 +156,23 @@
             gather_hop(r, 0, ch).start()
             hand_over(r, ch).start()
 
-    def forward(w, x):
+            @pl.when((r == final) & longer)
+            def _():
+                near(ch).start()
+
+    def forward(w, x, parted=False):
         t, r = x // RW, w * RW + lax.rem(x, RW)
         ch = mine(t)
         gather_hop(r, t, ch).wait_recv()
 
-        @pl.when(t < chips - 2)
+        @pl.when((t < chips - 2) & jnp.logical_not(parted))
         def _():
             gather_hop(r, t + 1, ch).start()
+
+        if parted is not False:
+            @pl.when(parted)
+            def _():
+                final_hop(ch).start()
 
         hand_over(r, ch).start()
 
@@ -303,10 +325,22 @@
                     load_g((w + 2) * RW - 1, nth(q)).start()
 
     def rest(x, carry):
-        forward(waves - 1, x)
+        forward(waves - 1, x, (x == forwards - RW - 1) & longer)
         return carry
 
-    lax.fori_loop(0, forwards, rest, 0)
+    lax.fori_loop(0, forwards - 1, rest, 0)
+    ch = mine(chips - 2)
+
+    @pl.when(longer)
+    def _():
+        near(ch).wait_recv()
+        final_hop(ch).wait_recv()
+
+    @pl.when(jnp.logical_not(longer))
+    def _():
+        gather_hop(final, chips - 2, ch).wait_recv()
+
+    hand_over(final, ch).start()
 
     for i in range(steps - DS, steps):
         swap(i).wait_send()
@@ -327,7 +361,7 @@
         rounds = matrices * ff // NB // chips
         hops = rounds * (chips - 1)
         bf16, f32 = jnp.bfloat16, jnp.float32
-        sems = [AS, AS, RW * chips, DS, DS, 1, 1, rounds * chips, 1, 1]
+        sems = [AS, AS, RW * chips, DS, DS, 1, 1, rounds * chips, 1, 1, 1]
         return pl.pallas_call(
             functools.partial(kernel, chips),
             out_shape=pltpu.MemorySpace.VMEM((matrices, d, ff), bf16),

time: 80.6 us -> 79.3 us (0.984)
  Pallas kernels: 77.3 us -> 76 us
    pallas_call x1, Pallas kernels: 77.3 us -> 76 us  [one(): pl.pallas_call(functools.partial(kernel, chips), out_shape=pltpu.MemorySp...]
where the time goes in v4:
time: 79.3 us; the launch traced here: 79.2 us
  Pallas kernels  76 us (96%)
  local copies, waits for them, and re-layouts  3.22 us (4%)
    pallas_call x1, Pallas kernels, one(): pl.pallas_call(functools.partial(kernel, chips), out_shape=pltpu.MemorySp...  76 us
    unnamed x1, local copies, waits for them, and re-layouts  3.22 us

profile of v4, /device:TPU:113, one launch (start us, length us, event | category | flops | bytes accessed | tf_op | source)
XLA Modules:
  0.0 79.2 jit_solution(3207309807908599980)
XLA Ops:
  0.0 76.0 %shard_map.28 = bf16[4,640,1536]{2,1,0:T(8,128)(2,1)S(1)} custom-call(bf16[4,4096,640]{2,1,0:T(8,128)(2,1)} %bitcast.3, bf16[4,4096,1536]{2,1,0:T(8,128)(2,1)} %bitcast.2), custom_call_target="tpu_custom_call" | custom-call | tf_op jit(solution)/shard_map/pallas_call | solution.py:365
  76.0 3.2 %copy.4 = bf16[4,640,1536]{2,1,0:T(8,128)(2,1)} copy(bf16[4,640,1536]{2,1,0:T(8,128)(2,1)S(1)} %shard_map.28) | data formatting | bytes 15728640
